TPU v7x, 128 devices: a whole 4x4x4 slice. The times are simulated.
128 devices in a mesh: hst: 2 (over core), row: 4 (over x), col: 16 (over z, y).
Axes of the slice: x: 4, y: 4, z: 4, core: 2. Of those that a mesh axis runs over, the one named last changes fastest.
Arguments:
- tables: bfloat16 [1024, 1024, 128], P(('hst', 'row', 'col')), may hold values from -6 to 6
- indices: int32 [1024, 2048, 4], P(('hst', 'row', 'col')), may hold values from 0 to 1023
- lengths: int32 [1024, 2048], P(('hst', 'row', 'col')), may hold values from 1 to 4, as said below
- table_slot: int32 [1024], replicated, may hold values from 0 to 1023, each once
- dense_feature: bfloat16 [2048, 128], P(('hst', 'row', 'col')), may hold values from -48 to 48
- left_proj: bfloat16 [128, 1025], replicated, may hold values from -0.1875 to 0.1875
- right_proj: bfloat16 [128, 1025], replicated, may hold values from -0.1875 to 0.1875
Outputs:
- interaction: bfloat16 [2048, 16384], P(('hst', 'row', 'col'))
Inputs may be any that keep to these rules, and one draw needn't show every extreme that they name: Each bag uses its first lengths ids; some bag holds 4 ids.
All inputs are finite; a program needn't handle non-finite values.
Results may differ from a plain program's by a relative error of at most 0.0063.
Values may be sent and summed in bfloat16 or wider, within the bound.
A program may use at most 64 MiB of HBM per device.

v0:
```python
import jax
import jax.numpy as jnp
from jax import lax
from jax.sharding import PartitionSpec as P


def pool_table(table, row_ids, bag_lens, bag_size):
    all_samples = row_ids.shape[0]
    table_rows = table.shape[0]
    feature_width = table.shape[1]
    block = 512
    row_iota = lax.broadcasted_iota(jnp.int32, (1, table_rows), 1)

    def one_block(items):
        block_ids, block_lens = items

        def add_ids(position, counts):
            chosen_ids = lax.dynamic_index_in_dim(block_ids, position, 1, keepdims=False)
            hit = (chosen_ids[:, None] == row_iota) & (position < block_lens)[:, None]
            return counts + hit.astype(jnp.bfloat16)

        counts = jnp.zeros((block, table_rows), jnp.bfloat16)
        counts = lax.fori_loop(0, bag_size, add_ids, counts)
        return jnp.dot(counts, table, preferred_element_type=jnp.float32).astype(jnp.bfloat16)

    grouped_ids = row_ids.reshape(all_samples // block, block, row_ids.shape[1])
    grouped_lens = bag_lens.reshape(all_samples // block, block)
    pooled = lax.map(one_block, (grouped_ids, grouped_lens))
    return pooled.reshape(all_samples, feature_width)


def shards(tables, indices, lengths, table_slot, dense_feature, left_proj, right_proj):
    tab_dev, all_samples, bag_size = indices.shape
    feature_width = tables.shape[2]
    devices = lax.axis_size(("hst", "row", "col"))
    own_samples = all_samples // devices
    proj_rows = left_proj.shape[0]
    tables_total = left_proj.shape[1] - 1
    pooled = lax.map(
        lambda items: pool_table(items[0], items[1], items[2], bag_size), (tables, indices, lengths)
    )
    blocks = pooled.reshape(tab_dev, devices, own_samples, feature_width)
    positions = jnp.arange(tables_total, dtype=jnp.int32)
    within = positions % tab_dev
    source = positions // tab_dev
    slot_here = source * tab_dev + within
    projections = jnp.concatenate([left_proj, right_proj], axis=0)
    selector = (table_slot[:, None] == slot_here[None, :]).astype(jnp.bfloat16)
    proj_here = jnp.dot(projections[:, 1:], selector, preferred_element_type=jnp.float32).astype(
        jnp.bfloat16
    )
    received = lax.all_to_all(
        blocks, ("hst", "row", "col"), split_axis=1, concat_axis=0, tiled=True
    )
    count = received.shape[2]
    flattened = received.reshape(tables_total, count * feature_width)
    mixed_all = jnp.dot(proj_here, flattened, preferred_element_type=jnp.float32)
    mixed_all = mixed_all.reshape(2 * proj_rows, count, feature_width)
    dense_column = projections[:, 0].astype(jnp.float32)
    mixed_all = mixed_all + dense_column[:, None, None] * dense_feature[None].astype(jnp.float32)
    mixed_all = mixed_all.astype(jnp.bfloat16)
    left_side = mixed_all[:proj_rows]
    right_side = mixed_all[proj_rows:]
    products = jnp.einsum("kbe,lbe->bkl", left_side, right_side, preferred_element_type=jnp.float32)
    products = products * (1.0 / feature_width)
    return products.reshape(own_samples, proj_rows * proj_rows).astype(jnp.bfloat16)


def solution(mesh):
    in_specs = (
        P(("hst", "row", "col"), None, None),
        P(("hst", "row", "col"), None, None),
        P(("hst", "row", "col"), None),
        P(),
        P(("hst", "row", "col"), None),
        P(),
        P(),
    )
    out_specs = P(("hst", "row", "col"), None)
    return jax.shard_map(shards, mesh=mesh, in_specs=in_specs, out_specs=out_specs, check_vma=False)
```

profile of v0, /device:TPU:34, one launch (start us, length us, event | category | flops | bytes accessed | tf_op | source)
XLA Modules:
  0.0 217.0 jit_solution(7283805805666844912)
XLA Ops:
  0.0 125.8 %while.38 = (s32[]{:T(128)}, bf16[8,2048,128]{2,1,0:T(8,128)(2,1)}, s32[8,2048,4]{1,2,0:T(4,128)}, s32[8,2048]{1,0:T(8,128)}, bf16[8,1024,128]{2,1,0:T(8,128)(2,...) while((s32[]{:T(128)}, bf16[8,2048,128]{2,1,0:T(8,128)(2,1)}, ...), condition=%wide.region_5.6_spmd, body=%wide.region_0.5_spmd.sunk | while | flops 138478080 | bytes 5248493 | solution.py:39
  2.6 12.3 %while.39 = (s32[]{:T(128)}, bf16[4,512,128]{2,1,0:T(8,128)(2,1)S(1)}, s32[4,512,4]{1,2,0:T(4,128)S(1)}, s32[4,512]{1,0:T(4,128)S(1)}, bf16[1024,128]{1,0:T(8,12...) while((s32[]{:T(128)}, bf16[4,512,128]{2,1,0:T(8,128)(2,1)S(1)}, ...), condition=%wide.region_4.4_spmd.clone, body=%wide.region_1.3_spmd.clone.sunk | while | flops 138478080 | bytes 3577112 | solution.py:28
  2.7 2.5 %while.40 = (s32[]{:T(128)}, bf16[512,1024]{1,0:T(8,128)(2,1)S(1)}, s32[512,4]{0,1:T(4,128)S(1)}, s32[1,1024]{1,0:T(1,128)S(1)}, s32[512]{0:T(512)S(1)}, /*index=5*/s32[]{:T(128)}, s32[]{:T(128)}) while((s32[]{:T(128)}, bf16[512,1024]{1,0:T(8,128)(2,1)S(1)}, s32[512,4]{0,1:T(4,128)S(1)}, s32[1,1024]{1,0:T(1,128)S(1)}, ...), condition=%wide.region_3.2_spmd.clone, body=%wide.region_2.1_spmd.clone.sunk | while | flops 4194819 | bytes 2110567 | solution.py:23
  5.8 2.5 %while.40 = (s32[]{:T(128)}, bf16[512,1024]{1,0:T(8,128)(2,1)S(1)}, s32[512,4]{0,1:T(4,128)S(1)}, s32[1,1024]{1,0:T(1,128)S(1)}, s32[512]{0:T(512)S(1)}, /*index=5*/s32[]{:T(128)}, s32[]{:T(128)}) while((s32[]{:T(128)}, bf16[512,1024]{1,0:T(8,128)(2,1)S(1)}, s32[512,4]{0,1:T(4,128)S(1)}, s32[1,1024]{1,0:T(1,128)S(1)}, ...), condition=%wide.region_3.2_spmd.clone, body=%wide.region_2.1_spmd.clone.sunk | while | flops 4194819 | bytes 2110567 | solution.py:23
  8.8 2.5 %while.40 = (s32[]{:T(128)}, bf16[512,1024]{1,0:T(8,128)(2,1)S(1)}, s32[512,4]{0,1:T(4,128)S(1)}, s32[1,1024]{1,0:T(1,128)S(1)}, s32[512]{0:T(512)S(1)}, /*index=5*/s32[]{:T(128)}, s32[]{:T(128)}) while((s32[]{:T(128)}, bf16[512,1024]{1,0:T(8,128)(2,1)S(1)}, s32[512,4]{0,1:T(4,128)S(1)}, s32[1,1024]{1,0:T(1,128)S(1)}, ...), condition=%wide.region_3.2_spmd.clone, body=%wide.region_2.1_spmd.clone.sunk | while | flops 4194819 | bytes 2110567 | solution.py:23
  11.9 2.5 %while.40 = (s32[]{:T(128)}, bf16[512,1024]{1,0:T(8,128)(2,1)S(1)}, s32[512,4]{0,1:T(4,128)S(1)}, s32[1,1024]{1,0:T(1,128)S(1)}, s32[512]{0:T(512)S(1)}, /*index=5*/s32[]{:T(128)}, s32[]{:T(128)}) while((s32[]{:T(128)}, bf16[512,1024]{1,0:T(8,128)(2,1)S(1)}, s32[512,4]{0,1:T(4,128)S(1)}, s32[1,1024]{1,0:T(1,128)S(1)}, ...), condition=%wide.region_3.2_spmd.clone, body=%wide.region_2.1_spmd.clone.sunk | while | flops 4194819 | bytes 2110567 | solution.py:23
  18.3 12.3 %while.39 = (s32[]{:T(128)}, bf16[4,512,128]{2,1,0:T(8,128)(2,1)S(1)}, s32[4,512,4]{1,2,0:T(4,128)S(1)}, s32[4,512]{1,0:T(4,128)S(1)}, bf16[1024,128]{1,0:T(8,12...) while((s32[]{:T(128)}, bf16[4,512,128]{2,1,0:T(8,128)(2,1)S(1)}, ...), condition=%wide.region_4.4_spmd.clone, body=%wide.region_1.3_spmd.clone.sunk | while | flops 138478080 | bytes 3577112 | solution.py:28
  18.4 2.5 %while.40 = (s32[]{:T(128)}, bf16[512,1024]{1,0:T(8,128)(2,1)S(1)}, s32[512,4]{0,1:T(4,128)S(1)}, s32[1,1024]{1,0:T(1,128)S(1)}, s32[512]{0:T(512)S(1)}, /*index=5*/s32[]{:T(128)}, s32[]{:T(128)}) while((s32[]{:T(128)}, bf16[512,1024]{1,0:T(8,128)(2,1)S(1)}, s32[512,4]{0,1:T(4,128)S(1)}, s32[1,1024]{1,0:T(1,128)S(1)}, ...), condition=%wide.region_3.2_spmd.clone, body=%wide.region_2.1_spmd.clone.sunk | while | flops 4194819 | bytes 2110567 | solution.py:23
  21.5 2.5 %while.40 = (s32[]{:T(128)}, bf16[512,1024]{1,0:T(8,128)(2,1)S(1)}, s32[512,4]{0,1:T(4,128)S(1)}, s32[1,1024]{1,0:T(1,128)S(1)}, s32[512]{0:T(512)S(1)}, /*index=5*/s32[]{:T(128)}, s32[]{:T(128)}) while((s32[]{:T(128)}, bf16[512,1024]{1,0:T(8,128)(2,1)S(1)}, s32[512,4]{0,1:T(4,128)S(1)}, s32[1,1024]{1,0:T(1,128)S(1)}, ...), condition=%wide.region_3.2_spmd.clone, body=%wide.region_2.1_spmd.clone.sunk | while | flops 4194819 | bytes 2110567 | solution.py:23
  24.5 2.5 %while.40 = (s32[]{:T(128)}, bf16[512,1024]{1,0:T(8,128)(2,1)S(1)}, s32[512,4]{0,1:T(4,128)S(1)}, s32[1,1024]{1,0:T(1,128)S(1)}, s32[512]{0:T(512)S(1)}, /*index=5*/s32[]{:T(128)}, s32[]{:T(128)}) while((s32[]{:T(128)}, bf16[512,1024]{1,0:T(8,128)(2,1)S(1)}, s32[512,4]{0,1:T(4,128)S(1)}, s32[1,1024]{1,0:T(1,128)S(1)}, ...), condition=%wide.region_3.2_spmd.clone, body=%wide.region_2.1_spmd.clone.sunk | while | flops 4194819 | bytes 2110567 | solution.py:23
  27.6 2.5 %while.40 = (s32[]{:T(128)}, bf16[512,1024]{1,0:T(8,128)(2,1)S(1)}, s32[512,4]{0,1:T(4,128)S(1)}, s32[1,1024]{1,0:T(1,128)S(1)}, s32[512]{0:T(512)S(1)}, /*index=5*/s32[]{:T(128)}, s32[]{:T(128)}) while((s32[]{:T(128)}, bf16[512,1024]{1,0:T(8,128)(2,1)S(1)}, s32[512,4]{0,1:T(4,128)S(1)}, s32[1,1024]{1,0:T(1,128)S(1)}, ...), condition=%wide.region_3.2_spmd.clone, body=%wide.region_2.1_spmd.clone.sunk | while | flops 4194819 | bytes 2110567 | solution.py:23
  34.1 12.3 %while.39 = (s32[]{:T(128)}, bf16[4,512,128]{2,1,0:T(8,128)(2,1)S(1)}, s32[4,512,4]{1,2,0:T(4,128)S(1)}, s32[4,512]{1,0:T(4,128)S(1)}, bf16[1024,128]{1,0:T(8,12...) while((s32[]{:T(128)}, bf16[4,512,128]{2,1,0:T(8,128)(2,1)S(1)}, ...), condition=%wide.region_4.4_spmd.clone, body=%wide.region_1.3_spmd.clone.sunk | while | flops 138478080 | bytes 3577112 | solution.py:28
  34.1 2.5 %while.40 = (s32[]{:T(128)}, bf16[512,1024]{1,0:T(8,128)(2,1)S(1)}, s32[512,4]{0,1:T(4,128)S(1)}, s32[1,1024]{1,0:T(1,128)S(1)}, s32[512]{0:T(512)S(1)}, /*index=5*/s32[]{:T(128)}, s32[]{:T(128)}) while((s32[]{:T(128)}, bf16[512,1024]{1,0:T(8,128)(2,1)S(1)}, s32[512,4]{0,1:T(4,128)S(1)}, s32[1,1024]{1,0:T(1,128)S(1)}, ...), condition=%wide.region_3.2_spmd.clone, body=%wide.region_2.1_spmd.clone.sunk | while | flops 4194819 | bytes 2110567 | solution.py:23
  37.2 2.5 %while.40 = (s32[]{:T(128)}, bf16[512,1024]{1,0:T(8,128)(2,1)S(1)}, s32[512,4]{0,1:T(4,128)S(1)}, s32[1,1024]{1,0:T(1,128)S(1)}, s32[512]{0:T(512)S(1)}, /*index=5*/s32[]{:T(128)}, s32[]{:T(128)}) while((s32[]{:T(128)}, bf16[512,1024]{1,0:T(8,128)(2,1)S(1)}, s32[512,4]{0,1:T(4,128)S(1)}, s32[1,1024]{1,0:T(1,128)S(1)}, ...), condition=%wide.region_3.2_spmd.clone, body=%wide.region_2.1_spmd.clone.sunk | while | flops 4194819 | bytes 2110567 | solution.py:23
  40.3 2.5 %while.40 = (s32[]{:T(128)}, bf16[512,1024]{1,0:T(8,128)(2,1)S(1)}, s32[512,4]{0,1:T(4,128)S(1)}, s32[1,1024]{1,0:T(1,128)S(1)}, s32[512]{0:T(512)S(1)}, /*index=5*/s32[]{:T(128)}, s32[]{:T(128)}) while((s32[]{:T(128)}, bf16[512,1024]{1,0:T(8,128)(2,1)S(1)}, s32[512,4]{0,1:T(4,128)S(1)}, s32[1,1024]{1,0:T(1,128)S(1)}, ...), condition=%wide.region_3.2_spmd.clone, body=%wide.region_2.1_spmd.clone.sunk | while | flops 4194819 | bytes 2110567 | solution.py:23
  43.3 2.5 %while.40 = (s32[]{:T(128)}, bf16[512,1024]{1,0:T(8,128)(2,1)S(1)}, s32[512,4]{0,1:T(4,128)S(1)}, s32[1,1024]{1,0:T(1,128)S(1)}, s32[512]{0:T(512)S(1)}, /*index=5*/s32[]{:T(128)}, s32[]{:T(128)}) while((s32[]{:T(128)}, bf16[512,1024]{1,0:T(8,128)(2,1)S(1)}, s32[512,4]{0,1:T(4,128)S(1)}, s32[1,1024]{1,0:T(1,128)S(1)}, ...), condition=%wide.region_3.2_spmd.clone, body=%wide.region_2.1_spmd.clone.sunk | while | flops 4194819 | bytes 2110567 | solution.py:23
  49.8 12.3 %while.39 = (s32[]{:T(128)}, bf16[4,512,128]{2,1,0:T(8,128)(2,1)S(1)}, s32[4,512,4]{1,2,0:T(4,128)S(1)}, s32[4,512]{1,0:T(4,128)S(1)}, bf16[1024,128]{1,0:T(8,12...) while((s32[]{:T(128)}, bf16[4,512,128]{2,1,0:T(8,128)(2,1)S(1)}, ...), condition=%wide.region_4.4_spmd.clone, body=%wide.region_1.3_spmd.clone.sunk | while | flops 138478080 | bytes 3577112 | solution.py:28
  49.9 2.5 %while.40 = (s32[]{:T(128)}, bf16[512,1024]{1,0:T(8,128)(2,1)S(1)}, s32[512,4]{0,1:T(4,128)S(1)}, s32[1,1024]{1,0:T(1,128)S(1)}, s32[512]{0:T(512)S(1)}, /*index=5*/s32[]{:T(128)}, s32[]{:T(128)}) while((s32[]{:T(128)}, bf16[512,1024]{1,0:T(8,128)(2,1)S(1)}, s32[512,4]{0,1:T(4,128)S(1)}, s32[1,1024]{1,0:T(1,128)S(1)}, ...), condition=%wide.region_3.2_spmd.clone, body=%wide.region_2.1_spmd.clone.sunk | while | flops 4194819 | bytes 2110567 | solution.py:23
  52.9 2.5 %while.40 = (s32[]{:T(128)}, bf16[512,1024]{1,0:T(8,128)(2,1)S(1)}, s32[512,4]{0,1:T(4,128)S(1)}, s32[1,1024]{1,0:T(1,128)S(1)}, s32[512]{0:T(512)S(1)}, /*index=5*/s32[]{:T(128)}, s32[]{:T(128)}) while((s32[]{:T(128)}, bf16[512,1024]{1,0:T(8,128)(2,1)S(1)}, s32[512,4]{0,1:T(4,128)S(1)}, s32[1,1024]{1,0:T(1,128)S(1)}, ...), condition=%wide.region_3.2_spmd.clone, body=%wide.region_2.1_spmd.clone.sunk | while | flops 4194819 | bytes 2110567 | solution.py:23
  56.0 2.5 %while.40 = (s32[]{:T(128)}, bf16[512,1024]{1,0:T(8,128)(2,1)S(1)}, s32[512,4]{0,1:T(4,128)S(1)}, s32[1,1024]{1,0:T(1,128)S(1)}, s32[512]{0:T(512)S(1)}, /*index=5*/s32[]{:T(128)}, s32[]{:T(128)}) while((s32[]{:T(128)}, bf16[512,1024]{1,0:T(8,128)(2,1)S(1)}, s32[512,4]{0,1:T(4,128)S(1)}, s32[1,1024]{1,0:T(1,128)S(1)}, ...), condition=%wide.region_3.2_spmd.clone, body=%wide.region_2.1_spmd.clone.sunk | while | flops 4194819 | bytes 2110567 | solution.py:23
  59.1 2.5 %while.40 = (s32[]{:T(128)}, bf16[512,1024]{1,0:T(8,128)(2,1)S(1)}, s32[512,4]{0,1:T(4,128)S(1)}, s32[1,1024]{1,0:T(1,128)S(1)}, s32[512]{0:T(512)S(1)}, /*index=5*/s32[]{:T(128)}, s32[]{:T(128)}) while((s32[]{:T(128)}, bf16[512,1024]{1,0:T(8,128)(2,1)S(1)}, s32[512,4]{0,1:T(4,128)S(1)}, s32[1,1024]{1,0:T(1,128)S(1)}, ...), condition=%wide.region_3.2_spmd.clone, body=%wide.region_2.1_spmd.clone.sunk | while | flops 4194819 | bytes 2110567 | solution.py:23
  65.5 12.3 %while.39 = (s32[]{:T(128)}, bf16[4,512,128]{2,1,0:T(8,128)(2,1)S(1)}, s32[4,512,4]{1,2,0:T(4,128)S(1)}, s32[4,512]{1,0:T(4,128)S(1)}, bf16[1024,128]{1,0:T(8,12...) while((s32[]{:T(128)}, bf16[4,512,128]{2,1,0:T(8,128)(2,1)S(1)}, ...), condition=%wide.region_4.4_spmd.clone, body=%wide.region_1.3_spmd.clone.sunk | while | flops 138478080 | bytes 3577112 | solution.py:28
  65.6 2.5 %while.40 = (s32[]{:T(128)}, bf16[512,1024]{1,0:T(8,128)(2,1)S(1)}, s32[512,4]{0,1:T(4,128)S(1)}, s32[1,1024]{1,0:T(1,128)S(1)}, s32[512]{0:T(512)S(1)}, /*index=5*/s32[]{:T(128)}, s32[]{:T(128)}) while((s32[]{:T(128)}, bf16[512,1024]{1,0:T(8,128)(2,1)S(1)}, s32[512,4]{0,1:T(4,128)S(1)}, s32[1,1024]{1,0:T(1,128)S(1)}, ...), condition=%wide.region_3.2_spmd.clone, body=%wide.region_2.1_spmd.clone.sunk | while | flops 4194819 | bytes 2110567 | solution.py:23
  68.7 2.5 %while.40 = (s32[]{:T(128)}, bf16[512,1024]{1,0:T(8,128)(2,1)S(1)}, s32[512,4]{0,1:T(4,128)S(1)}, s32[1,1024]{1,0:T(1,128)S(1)}, s32[512]{0:T(512)S(1)}, /*index=5*/s32[]{:T(128)}, s32[]{:T(128)}) while((s32[]{:T(128)}, bf16[512,1024]{1,0:T(8,128)(2,1)S(1)}, s32[512,4]{0,1:T(4,128)S(1)}, s32[1,1024]{1,0:T(1,128)S(1)}, ...), condition=%wide.region_3.2_spmd.clone, body=%wide.region_2.1_spmd.clone.sunk | while | flops 4194819 | bytes 2110567 | solution.py:23
  71.7 2.5 %while.40 = (s32[]{:T(128)}, bf16[512,1024]{1,0:T(8,128)(2,1)S(1)}, s32[512,4]{0,1:T(4,128)S(1)}, s32[1,1024]{1,0:T(1,128)S(1)}, s32[512]{0:T(512)S(1)}, /*index=5*/s32[]{:T(128)}, s32[]{:T(128)}) while((s32[]{:T(128)}, bf16[512,1024]{1,0:T(8,128)(2,1)S(1)}, s32[512,4]{0,1:T(4,128)S(1)}, s32[1,1024]{1,0:T(1,128)S(1)}, ...), condition=%wide.region_3.2_spmd.clone, body=%wide.region_2.1_spmd.clone.sunk | while | flops 4194819 | bytes 2110567 | solution.py:23
  74.8 2.5 %while.40 = (s32[]{:T(128)}, bf16[512,1024]{1,0:T(8,128)(2,1)S(1)}, s32[512,4]{0,1:T(4,128)S(1)}, s32[1,1024]{1,0:T(1,128)S(1)}, s32[512]{0:T(512)S(1)}, /*index=5*/s32[]{:T(128)}, s32[]{:T(128)}) while((s32[]{:T(128)}, bf16[512,1024]{1,0:T(8,128)(2,1)S(1)}, s32[512,4]{0,1:T(4,128)S(1)}, s32[1,1024]{1,0:T(1,128)S(1)}, ...), condition=%wide.region_3.2_spmd.clone, body=%wide.region_2.1_spmd.clone.sunk | while | flops 4194819 | bytes 2110567 | solution.py:23
  81.3 12.3 %while.39 = (s32[]{:T(128)}, bf16[4,512,128]{2,1,0:T(8,128)(2,1)S(1)}, s32[4,512,4]{1,2,0:T(4,128)S(1)}, s32[4,512]{1,0:T(4,128)S(1)}, bf16[1024,128]{1,0:T(8,12...) while((s32[]{:T(128)}, bf16[4,512,128]{2,1,0:T(8,128)(2,1)S(1)}, ...), condition=%wide.region_4.4_spmd.clone, body=%wide.region_1.3_spmd.clone.sunk | while | flops 138478080 | bytes 3577112 | solution.py:28
  81.3 2.5 %while.40 = (s32[]{:T(128)}, bf16[512,1024]{1,0:T(8,128)(2,1)S(1)}, s32[512,4]{0,1:T(4,128)S(1)}, s32[1,1024]{1,0:T(1,128)S(1)}, s32[512]{0:T(512)S(1)}, /*index=5*/s32[]{:T(128)}, s32[]{:T(128)}) while((s32[]{:T(128)}, bf16[512,1024]{1,0:T(8,128)(2,1)S(1)}, s32[512,4]{0,1:T(4,128)S(1)}, s32[1,1024]{1,0:T(1,128)S(1)}, ...), condition=%wide.region_3.2_spmd.clone, body=%wide.region_2.1_spmd.clone.sunk | while | flops 4194819 | bytes 2110567 | solution.py:23
  84.4 2.5 %while.40 = (s32[]{:T(128)}, bf16[512,1024]{1,0:T(8,128)(2,1)S(1)}, s32[512,4]{0,1:T(4,128)S(1)}, s32[1,1024]{1,0:T(1,128)S(1)}, s32[512]{0:T(512)S(1)}, /*index=5*/s32[]{:T(128)}, s32[]{:T(128)}) while((s32[]{:T(128)}, bf16[512,1024]{1,0:T(8,128)(2,1)S(1)}, s32[512,4]{0,1:T(4,128)S(1)}, s32[1,1024]{1,0:T(1,128)S(1)}, ...), condition=%wide.region_3.2_spmd.clone, body=%wide.region_2.1_spmd.clone.sunk | while | flops 4194819 | bytes 2110567 | solution.py:23
  87.5 2.5 %while.40 = (s32[]{:T(128)}, bf16[512,1024]{1,0:T(8,128)(2,1)S(1)}, s32[512,4]{0,1:T(4,128)S(1)}, s32[1,1024]{1,0:T(1,128)S(1)}, s32[512]{0:T(512)S(1)}, /*index=5*/s32[]{:T(128)}, s32[]{:T(128)}) while((s32[]{:T(128)}, bf16[512,1024]{1,0:T(8,128)(2,1)S(1)}, s32[512,4]{0,1:T(4,128)S(1)}, s32[1,1024]{1,0:T(1,128)S(1)}, ...), condition=%wide.region_3.2_spmd.clone, body=%wide.region_2.1_spmd.clone.sunk | while | flops 4194819 | bytes 2110567 | solution.py:23
  90.5 2.5 %while.40 = (s32[]{:T(128)}, bf16[512,1024]{1,0:T(8,128)(2,1)S(1)}, s32[512,4]{0,1:T(4,128)S(1)}, s32[1,1024]{1,0:T(1,128)S(1)}, s32[512]{0:T(512)S(1)}, /*index=5*/s32[]{:T(128)}, s32[]{:T(128)}) while((s32[]{:T(128)}, bf16[512,1024]{1,0:T(8,128)(2,1)S(1)}, s32[512,4]{0,1:T(4,128)S(1)}, s32[1,1024]{1,0:T(1,128)S(1)}, ...), condition=%wide.region_3.2_spmd.clone, body=%wide.region_2.1_spmd.clone.sunk | while | flops 4194819 | bytes 2110567 | solution.py:23
  97.0 12.3 %while.39 = (s32[]{:T(128)}, bf16[4,512,128]{2,1,0:T(8,128)(2,1)S(1)}, s32[4,512,4]{1,2,0:T(4,128)S(1)}, s32[4,512]{1,0:T(4,128)S(1)}, bf16[1024,128]{1,0:T(8,12...) while((s32[]{:T(128)}, bf16[4,512,128]{2,1,0:T(8,128)(2,1)S(1)}, ...), condition=%wide.region_4.4_spmd.clone, body=%wide.region_1.3_spmd.clone.sunk | while | flops 138478080 | bytes 3577112 | solution.py:28
  97.1 2.5 %while.40 = (s32[]{:T(128)}, bf16[512,1024]{1,0:T(8,128)(2,1)S(1)}, s32[512,4]{0,1:T(4,128)S(1)}, s32[1,1024]{1,0:T(1,128)S(1)}, s32[512]{0:T(512)S(1)}, /*index=5*/s32[]{:T(128)}, s32[]{:T(128)}) while((s32[]{:T(128)}, bf16[512,1024]{1,0:T(8,128)(2,1)S(1)}, s32[512,4]{0,1:T(4,128)S(1)}, s32[1,1024]{1,0:T(1,128)S(1)}, ...), condition=%wide.region_3.2_spmd.clone, body=%wide.region_2.1_spmd.clone.sunk | while | flops 4194819 | bytes 2110567 | solution.py:23
  100.1 2.5 %while.40 = (s32[]{:T(128)}, bf16[512,1024]{1,0:T(8,128)(2,1)S(1)}, s32[512,4]{0,1:T(4,128)S(1)}, s32[1,1024]{1,0:T(1,128)S(1)}, s32[512]{0:T(512)S(1)}, /*index=5*/s32[]{:T(128)}, s32[]{:T(128)}) while((s32[]{:T(128)}, bf16[512,1024]{1,0:T(8,128)(2,1)S(1)}, s32[512,4]{0,1:T(4,128)S(1)}, s32[1,1024]{1,0:T(1,128)S(1)}, ...), condition=%wide.region_3.2_spmd.clone, body=%wide.region_2.1_spmd.clone.sunk | while | flops 4194819 | bytes 2110567 | solution.py:23
  103.2 2.5 %while.40 = (s32[]{:T(128)}, bf16[512,1024]{1,0:T(8,128)(2,1)S(1)}, s32[512,4]{0,1:T(4,128)S(1)}, s32[1,1024]{1,0:T(1,128)S(1)}, s32[512]{0:T(512)S(1)}, /*index=5*/s32[]{:T(128)}, s32[]{:T(128)}) while((s32[]{:T(128)}, bf16[512,1024]{1,0:T(8,128)(2,1)S(1)}, s32[512,4]{0,1:T(4,128)S(1)}, s32[1,1024]{1,0:T(1,128)S(1)}, ...), condition=%wide.region_3.2_spmd.clone, body=%wide.region_2.1_spmd.clone.sunk | while | flops 4194819 | bytes 2110567 | solution.py:23
  106.3 2.5 %while.40 = (s32[]{:T(128)}, bf16[512,1024]{1,0:T(8,128)(2,1)S(1)}, s32[512,4]{0,1:T(4,128)S(1)}, s32[1,1024]{1,0:T(1,128)S(1)}, s32[512]{0:T(512)S(1)}, /*index=5*/s32[]{:T(128)}, s32[]{:T(128)}) while((s32[]{:T(128)}, bf16[512,1024]{1,0:T(8,128)(2,1)S(1)}, s32[512,4]{0,1:T(4,128)S(1)}, s32[1,1024]{1,0:T(1,128)S(1)}, ...), condition=%wide.region_3.2_spmd.clone, body=%wide.region_2.1_spmd.clone.sunk | while | flops 4194819 | bytes 2110567 | solution.py:23
  112.7 12.3 %while.39 = (s32[]{:T(128)}, bf16[4,512,128]{2,1,0:T(8,128)(2,1)S(1)}, s32[4,512,4]{1,2,0:T(4,128)S(1)}, s32[4,512]{1,0:T(4,128)S(1)}, bf16[1024,128]{1,0:T(8,12...) while((s32[]{:T(128)}, bf16[4,512,128]{2,1,0:T(8,128)(2,1)S(1)}, ...), condition=%wide.region_4.4_spmd.clone, body=%wide.region_1.3_spmd.clone.sunk | while | flops 138478080 | bytes 3577112 | solution.py:28
  112.8 2.5 %while.40 = (s32[]{:T(128)}, bf16[512,1024]{1,0:T(8,128)(2,1)S(1)}, s32[512,4]{0,1:T(4,128)S(1)}, s32[1,1024]{1,0:T(1,128)S(1)}, s32[512]{0:T(512)S(1)}, /*index=5*/s32[]{:T(128)}, s32[]{:T(128)}) while((s32[]{:T(128)}, bf16[512,1024]{1,0:T(8,128)(2,1)S(1)}, s32[512,4]{0,1:T(4,128)S(1)}, s32[1,1024]{1,0:T(1,128)S(1)}, ...), condition=%wide.region_3.2_spmd.clone, body=%wide.region_2.1_spmd.clone.sunk | while | flops 4194819 | bytes 2110567 | solution.py:23
  115.9 2.5 %while.40 = (s32[]{:T(128)}, bf16[512,1024]{1,0:T(8,128)(2,1)S(1)}, s32[512,4]{0,1:T(4,128)S(1)}, s32[1,1024]{1,0:T(1,128)S(1)}, s32[512]{0:T(512)S(1)}, /*index=5*/s32[]{:T(128)}, s32[]{:T(128)}) while((s32[]{:T(128)}, bf16[512,1024]{1,0:T(8,128)(2,1)S(1)}, s32[512,4]{0,1:T(4,128)S(1)}, s32[1,1024]{1,0:T(1,128)S(1)}, ...), condition=%wide.region_3.2_spmd.clone, body=%wide.region_2.1_spmd.clone.sunk | while | flops 4194819 | bytes 2110567 | solution.py:23
  118.9 2.5 %while.40 = (s32[]{:T(128)}, bf16[512,1024]{1,0:T(8,128)(2,1)S(1)}, s32[512,4]{0,1:T(4,128)S(1)}, s32[1,1024]{1,0:T(1,128)S(1)}, s32[512]{0:T(512)S(1)}, /*index=5*/s32[]{:T(128)}, s32[]{:T(128)}) while((s32[]{:T(128)}, bf16[512,1024]{1,0:T(8,128)(2,1)S(1)}, s32[512,4]{0,1:T(4,128)S(1)}, s32[1,1024]{1,0:T(1,128)S(1)}, ...), condition=%wide.region_3.2_spmd.clone, body=%wide.region_2.1_spmd.clone.sunk | while | flops 4194819 | bytes 2110567 | solution.py:23
  122.0 2.5 %while.40 = (s32[]{:T(128)}, bf16[512,1024]{1,0:T(8,128)(2,1)S(1)}, s32[512,4]{0,1:T(4,128)S(1)}, s32[1,1024]{1,0:T(1,128)S(1)}, s32[512]{0:T(512)S(1)}, /*index=5*/s32[]{:T(128)}, s32[]{:T(128)}) while((s32[]{:T(128)}, bf16[512,1024]{1,0:T(8,128)(2,1)S(1)}, s32[512,4]{0,1:T(4,128)S(1)}, s32[1,1024]{1,0:T(1,128)S(1)}, ...), condition=%wide.region_3.2_spmd.clone, body=%wide.region_2.1_spmd.clone.sunk | while | flops 4194819 | bytes 2110567 | solution.py:23
  125.8 5.4 %copy.9 = bf16[8,128,16,128]{3,2,0,1:T(8,128)(2,1)} copy(bf16[8,128,16,128]{3,2,1,0:T(8,128)(2,1)} %bitcast.66) | data formatting | bytes 8388608 | tf_op jit(solution)/shard_map/reshape | solution.py:42
  131.2 10.7 %all-to-all-start = ((bf16[8,128,16,128]{3,2,0,1:T(8,128)(2,1)}), bf16[8,128,16,128]{3,2,0,1:T(8,128)(2,1)}, u32[]{:S(2)}, u32[]{:S(2)}) async-start(bf16[8,128,16,128]{3,2,0,1:T(8,128)(2,1)} %copy.9), calls=%async_computation | async-start | bytes 8388608 | tf_op jit(solution)/shard_map/all_to_all | solution.py:52
  142.1 56.2 %all-to-all-done = bf16[8,128,16,128]{3,2,0,1:T(8,128)(2,1)} async-done(((bf16[8,128,16,128]{3,2,0,1:T(8,128)(2,1)}), bf16[8,128,16,128]{3,2,0,1:T(8,128)(2,1)}, u32[]{:S(2)}, u32[]{:S(2)}) %all-to-all-start) | async-done | bytes 4194336 | tf_op jit(solution)/shard_map/all_to_all | solution.py:52
  198.3 6.3 %copy.15 = bf16[128,8,16,128]{3,1,2,0:T(8,128)(2,1)} copy(bf16[128,8,16,128]{3,2,1,0:T(8,128)(2,1)} %bitcast.18) | data formatting | bytes 8388608
  204.6 6.4 %copy.10 = bf16[2048,1024]{1,0:T(8,128)(2,1)} copy(bf16[2048,1024]{0,1:T(8,128)(2,1)} %bitcast.64) | data formatting | bytes 8388608 | tf_op jit(solution)/shard_map/dot_general | solution.py:57
  211.0 4.4 %add_convert_fusion = bf16[256,16,128]{2,0,1:T(8,128)(2,1)S(1)} fusion(bf16[16,128,1024]{2,1,0:T(8,128)(2,1)} %bitcast.67, f32[16,128]{1,0:T(8,128)S(1)} %convert_element_type.40, f32[256]{0:T(256)S(1)} %bitcast.70, s32[1024]{0:T(1024)S(1)} %fusion.29, s32[1024]{0:T(1024)S(1)} %copy-done.3, bf16[256,1025]{0,1:T(8,128)(2,1)S(1)} %constant_dynamic-update-slice_fusion), kind=kOutput, calls=%fused_computation.17 | convolution fusion | flops 1613496320 | bytes 5784576 | tf_op jit(solution)/shard_map/dot_general | solution.py:57
  215.9 1.1 copy.16
  (607 shorter events, 119.4 us)
Async XLA Ops:
  131.2 10.7 %copy-start.2 = (bf16[16,128]{1,0:T(8,128)(2,1)S(1)}, bf16[16,128]{1,0:T(8,128)(2,1)}, u32[]{:S(2)}) copy-start(bf16[16,128]{1,0:T(8,128)(2,1)} %param.17) | copy-start | bytes 12292
  131.2 10.7 %copy-start = (bf16[128,1025]{0,1:T(8,128)(2,1)S(1)}, bf16[128,1025]{0,1:T(8,128)(2,1)}, u32[]{:S(2)}) copy-start(bf16[128,1025]{0,1:T(8,128)(2,1)} %param.18) | copy-start | bytes 787204
  131.2 10.8 %copy-start.1 = (bf16[128,1025]{0,1:T(8,128)(2,1)S(1)}, bf16[128,1025]{0,1:T(8,128)(2,1)}, u32[]{:S(2)}) copy-start(bf16[128,1025]{0,1:T(8,128)(2,1)} %param.19) | copy-start | bytes 787204
  131.2 67.1 %all-to-all-start = ((bf16[8,128,16,128]{3,2,0,1:T(8,128)(2,1)}), bf16[8,128,16,128]{3,2,0,1:T(8,128)(2,1)}, u32[]{:S(2)}, u32[]{:S(2)}) async-start(bf16[8,128,16,128]{3,2,0,1:T(8,128)(2,1)} %copy.9), calls=%async_computation | async-start | bytes 8388608 | tf_op jit(solution)/shard_map/all_to_all | solution.py:52
  204.6 6.4 %copy-start.3 = (s32[1024]{0:T(1024)S(1)}, s32[1024]{0:T(1024)}, u32[]{:S(2)}) copy-start(s32[1024]{0:T(1024)} %param.16) | copy-start | bytes 12292
where the time goes:
time: 219 us; the launch traced here: 217 us
  other arithmetic  73.6 us (34%)
  waiting for transfers between devices  56.2 us (26%)
  local copies, waits for them, and re-layouts  48.8 us (22%)
  matrix products  20.5 us (9%)
  starting transfers between devices  10.7 us (5%)
  loops' own time  7.05 us (3%)
    add x128, other arithmetic, add_ids(): return counts + hit.astype(jnp.bfloat16)  72.8 us
    all_to_all x1, waiting for transfers between devices, shards(): lax.all_to_all(blocks, ('hst', 'row', 'col'), split_axis=1, concat_axis=0...  56.2 us
    dot_general x32, matrix products, one_block(): jnp.dot(counts, table, preferred_element_type=jnp.float32)  15.7 us
    dynamic_slice x16, local copies, waits for them, and re-layouts, shards(): lax.map(lambda items: pool_table(items[0], items[1], items[2], bag_size),...  13 us
    all_to_all x1, starting transfers between devices, shards(): lax.all_to_all(blocks, ('hst', 'row', 'col'), split_axis=1, concat_axis=0...  10.7 us
    squeeze x8, local copies, waits for them, and re-layouts, shards(): lax.map(lambda items: pool_table(items[0], items[1], items[2], bag_size),...  7.79 us
    unnamed x11, local copies, waits for them, and re-layouts  7.48 us
    dynamic_update_slice x8, local copies, waits for them, and re-layouts, shards(): lax.map(lambda items: pool_table(items[0], items[1], items[2], bag_size),...  6.71 us
  transfers between devices with their start and end apart: 1, of which 1 were waited for; matrix products, arithmetic and copies ran while one was open for 0% of the time, Pallas kernels for 0%

commit v1 on v0

--- a/solution.py
+++ b/solution.py
@@ -49,8 +49,14 @@
     proj_here = jnp.dot(projections[:, 1:], selector, preferred_element_type=jnp.float32).astype(
         jnp.bfloat16
     )
-    received = lax.all_to_all(
-        blocks, ("hst", "row", "col"), split_axis=1, concat_axis=0, tiled=True
+    received = jnp.concatenate(
+        lax.all_to_all(
+            jnp.stack(jnp.split(blocks, lax.axis_size(("hst", "row", "col")), axis=1)),
+            ("hst", "row", "col"),
+            0,
+            0,
+        ),
+        axis=0,
     )
     count = received.shape[2]
     flattened = received.reshape(tables_total, count * feature_width)

time: 219 us -> 344 us (1.57); the launches traced: 217 us -> 338 us
  local copies, waits for them, and re-layouts: 48.8 us -> 170 us
    unnamed x11 -> x140, local copies, waits for them, and re-layouts: 7.48 us -> 133 us
    reshape x1 -> x0, local copies, waits for them, and re-layouts: 5.4 us -> none  [shards(): blocks = pooled.reshape(tab_dev, devices, own_samples, feature_width)]
where the time goes in v1:
time: 344 us; the launch traced here: 338 us
  local copies, waits for them, and re-layouts  170 us (49%)
  other arithmetic  73.6 us (21%)
  waiting for transfers between devices  56.2 us (16%)
  matrix products  20.5 us (6%)
  starting transfers between devices  10.7 us (3%)
  loops' own time  7.11 us (2%)
    unnamed x140, local copies, waits for them, and re-layouts  133 us
    add x128, other arithmetic, add_ids(): return counts + hit.astype(jnp.bfloat16)  72.8 us
    all_to_all x1, waiting for transfers between devices, shards(): lax.all_to_all(jnp.stack(jnp.split(blocks, lax.axis_size(('hst', 'row', '...  56.2 us
    dot_general x32, matrix products, one_block(): jnp.dot(counts, table, preferred_element_type=jnp.float32)  15.7 us
    dynamic_slice x16, local copies, waits for them, and re-layouts, shards(): lax.map(lambda items: pool_table(items[0], items[1], items[2], bag_size),...  13.1 us
    all_to_all x1, starting transfers between devices, shards(): lax.all_to_all(jnp.stack(jnp.split(blocks, lax.axis_size(('hst', 'row', '...  10.7 us
    squeeze x8, local copies, waits for them, and re-layouts, shards(): lax.map(lambda items: pool_table(items[0], items[1], items[2], bag_size),...  7.73 us
  transfers between devices with their start and end apart: 1, of which 1 were waited for; matrix products, arithmetic and copies ran while one was open for 0% of the time, Pallas kernels for 0%

profile of v1, /device:TPU:34, one launch (start us, length us, event | category | flops | bytes accessed | tf_op | source)
XLA Modules:
  0.0 337.8 jit_solution(10602668357508147076)
XLA Ops:
  0.0 125.9 %while.38 = (s32[]{:T(128)}, bf16[8,2048,128]{2,1,0:T(8,128)(2,1)}, s32[8,2048,4]{1,2,0:T(4,128)}, s32[8,2048]{1,0:T(8,128)}, bf16[8,1024,128]{2,1,0:T(8,128)(2,...) while((s32[]{:T(128)}, bf16[8,2048,128]{2,1,0:T(8,128)(2,1)}, ...), condition=%wide.region_5.6_spmd, body=%wide.region_0.5_spmd.sunk | while | flops 138478080 | bytes 5248977 | solution.py:39
  2.6 12.3 %while.39 = (s32[]{:T(128)}, bf16[4,512,128]{2,1,0:T(8,128)(2,1)S(1)}, s32[4,512,4]{1,2,0:T(4,128)S(1)}, s32[4,512]{1,0:T(4,128)S(1)}, bf16[1024,128]{1,0:T(8,12...) while((s32[]{:T(128)}, bf16[4,512,128]{2,1,0:T(8,128)(2,1)S(1)}, ...), condition=%wide.region_4.4_spmd.clone, body=%wide.region_1.3_spmd.clone.sunk | while | flops 138478080 | bytes 3577096 | solution.py:28
  2.7 2.5 while.40
  5.8 2.5 while.40
  8.8 2.5 while.40
  11.9 2.5 while.40
  18.4 12.3 %while.39 = (s32[]{:T(128)}, bf16[4,512,128]{2,1,0:T(8,128)(2,1)S(1)}, s32[4,512,4]{1,2,0:T(4,128)S(1)}, s32[4,512]{1,0:T(4,128)S(1)}, bf16[1024,128]{1,0:T(8,12...) while((s32[]{:T(128)}, bf16[4,512,128]{2,1,0:T(8,128)(2,1)S(1)}, ...), condition=%wide.region_4.4_spmd.clone, body=%wide.region_1.3_spmd.clone.sunk | while | flops 138478080 | bytes 3577096 | solution.py:28
  18.4 2.5 while.40
  21.5 2.5 while.40
  24.6 2.5 while.40
  27.6 2.5 while.40
  34.1 12.3 %while.39 = (s32[]{:T(128)}, bf16[4,512,128]{2,1,0:T(8,128)(2,1)S(1)}, s32[4,512,4]{1,2,0:T(4,128)S(1)}, s32[4,512]{1,0:T(4,128)S(1)}, bf16[1024,128]{1,0:T(8,12...) while((s32[]{:T(128)}, bf16[4,512,128]{2,1,0:T(8,128)(2,1)S(1)}, ...), condition=%wide.region_4.4_spmd.clone, body=%wide.region_1.3_spmd.clone.sunk | while | flops 138478080 | bytes 3577096 | solution.py:28
  34.2 2.5 while.40
  37.2 2.5 while.40
  40.3 2.5 while.40
  43.4 2.5 while.40
  49.8 12.3 %while.39 = (s32[]{:T(128)}, bf16[4,512,128]{2,1,0:T(8,128)(2,1)S(1)}, s32[4,512,4]{1,2,0:T(4,128)S(1)}, s32[4,512]{1,0:T(4,128)S(1)}, bf16[1024,128]{1,0:T(8,12...) while((s32[]{:T(128)}, bf16[4,512,128]{2,1,0:T(8,128)(2,1)S(1)}, ...), condition=%wide.region_4.4_spmd.clone, body=%wide.region_1.3_spmd.clone.sunk | while | flops 138478080 | bytes 3577096 | solution.py:28
  49.9 2.5 while.40
  53.0 2.5 while.40
  56.0 2.5 while.40
  59.1 2.5 while.40
  65.6 12.3 %while.39 = (s32[]{:T(128)}, bf16[4,512,128]{2,1,0:T(8,128)(2,1)S(1)}, s32[4,512,4]{1,2,0:T(4,128)S(1)}, s32[4,512]{1,0:T(4,128)S(1)}, bf16[1024,128]{1,0:T(8,12...) while((s32[]{:T(128)}, bf16[4,512,128]{2,1,0:T(8,128)(2,1)S(1)}, ...), condition=%wide.region_4.4_spmd.clone, body=%wide.region_1.3_spmd.clone.sunk | while | flops 138478080 | bytes 3577096 | solution.py:28
  65.6 2.5 while.40
  68.7 2.5 while.40
  71.8 2.5 while.40
  74.8 2.5 while.40
  81.3 12.3 %while.39 = (s32[]{:T(128)}, bf16[4,512,128]{2,1,0:T(8,128)(2,1)S(1)}, s32[4,512,4]{1,2,0:T(4,128)S(1)}, s32[4,512]{1,0:T(4,128)S(1)}, bf16[1024,128]{1,0:T(8,12...) while((s32[]{:T(128)}, bf16[4,512,128]{2,1,0:T(8,128)(2,1)S(1)}, ...), condition=%wide.region_4.4_spmd.clone, body=%wide.region_1.3_spmd.clone.sunk | while | flops 138478080 | bytes 3577096 | solution.py:28
  81.4 2.5 while.40
  84.4 2.5 while.40
  87.5 2.5 while.40
  90.6 2.5 while.40
  97.0 12.3 %while.39 = (s32[]{:T(128)}, bf16[4,512,128]{2,1,0:T(8,128)(2,1)S(1)}, s32[4,512,4]{1,2,0:T(4,128)S(1)}, s32[4,512]{1,0:T(4,128)S(1)}, bf16[1024,128]{1,0:T(8,12...) while((s32[]{:T(128)}, bf16[4,512,128]{2,1,0:T(8,128)(2,1)S(1)}, ...), condition=%wide.region_4.4_spmd.clone, body=%wide.region_1.3_spmd.clone.sunk | while | flops 138478080 | bytes 3577096 | solution.py:28
  97.1 2.5 while.40
  100.2 2.5 while.40
  103.2 2.5 while.40
  106.3 2.5 while.40
  112.8 12.3 %while.39 = (s32[]{:T(128)}, bf16[4,512,128]{2,1,0:T(8,128)(2,1)S(1)}, s32[4,512,4]{1,2,0:T(4,128)S(1)}, s32[4,512]{1,0:T(4,128)S(1)}, bf16[1024,128]{1,0:T(8,12...) while((s32[]{:T(128)}, bf16[4,512,128]{2,1,0:T(8,128)(2,1)S(1)}, ...), condition=%wide.region_4.4_spmd.clone, body=%wide.region_1.3_spmd.clone.sunk | while | flops 138478080 | bytes 3577096 | solution.py:28
  112.8 2.5 while.40
  115.9 2.5 while.40
  119.0 2.5 while.40
  122.0 2.5 while.40
  125.9 1.5 constant_dynamic-update-slice_fusion.129
  176.4 1.4 constant_dynamic-update-slice_fusion.92
  252.1 10.7 %all-to-all-start = ((bf16[128,8,1,16,128]{4,3,1,2,0:T(8,128)(2,1)}), bf16[128,8,1,16,128]{4,3,1,2,0:T(8,128)(2,1)}, u32[]{:S(2)}, u32[]{:S(2)}) async-start(bf16[128,8,1,16,128]{4,3,1,2,0:T(8,128)(2,1)} %constant_dynamic-update-slice_fusion.2), calls=%async_computation | async-start | bytes 8388608 | tf_op jit(solution)/shard_map/all_to_all | solution.py:53
  262.9 56.2 %all-to-all-done = bf16[128,8,1,16,128]{4,3,1,2,0:T(8,128)(2,1)} async-done(((bf16[128,8,1,16,128]{4,3,1,2,0:T(8,128)(2,1)}), bf16[128,8,1,16,128]{4,3,1,2,0:T(8,128)(2,1)}, u32[]{:S(2)}, u32[]{:S(2)}) %all-to-all-start) | async-done | bytes 4194336 | tf_op jit(solution)/shard_map/all_to_all | solution.py:53
  319.2 6.3 %copy.525 = bf16[128,8,16,128]{3,1,2,0:T(8,128)(2,1)} copy(bf16[128,8,16,128]{3,2,1,0:T(8,128)(2,1)} %bitcast.397) | data formatting | bytes 8388608
  325.5 6.4 %copy.393 = bf16[2048,1024]{1,0:T(8,128)(2,1)} copy(bf16[2048,1024]{0,1:T(8,128)(2,1)} %bitcast.827) | data formatting | bytes 8388608 | tf_op jit(solution)/shard_map/dot_general | solution.py:63
  331.9 4.4 %add_convert_fusion = bf16[256,16,128]{2,0,1:T(8,128)(2,1)S(1)} fusion(bf16[16,128,1024]{2,1,0:T(8,128)(2,1)} %bitcast.829, f32[16,128]{1,0:T(8,128)S(1)} %convert_element_type.40, f32[256]{0:T(256)S(1)} %bitcast.960, s32[1024]{0:T(1024)S(1)} %fusion.29, s32[1024]{0:T(1024)S(1)} %copy-done.4, bf16[256,1025]{0,1:T(8,128)(2,1)S(1)} %constant_dynamic-update-slice_fusion), kind=kOutput, calls=%fused_computation.17 | convolution fusion | flops 1613496320 | bytes 5784576 | tf_op jit(solution)/shard_map/dot_general | solution.py:63
  (736 shorter events, 243.8 us)
Async XLA Ops:
  125.9 87.4 %copy-start = (bf16[8,2048,128]{2,1,0:T(8,128)(2,1)S(1)}, bf16[8,2048,128]{2,1,0:T(8,128)(2,1)}, u32[]{:S(2)}) copy-start(bf16[8,2048,128]{2,1,0:T(8,128)(2,1)} %get-tuple-element.158) | copy-start | bytes 12582916
  252.1 10.7 %copy-start.3 = (bf16[16,128]{1,0:T(8,128)(2,1)S(1)}, bf16[16,128]{1,0:T(8,128)(2,1)}, u32[]{:S(2)}) copy-start(bf16[16,128]{1,0:T(8,128)(2,1)} %param.17) | copy-start | bytes 12292
  252.1 10.7 %copy-start.1 = (bf16[128,1025]{0,1:T(8,128)(2,1)S(1)}, bf16[128,1025]{0,1:T(8,128)(2,1)}, u32[]{:S(2)}) copy-start(bf16[128,1025]{0,1:T(8,128)(2,1)} %param.18) | copy-start | bytes 787204
  252.1 10.8 %copy-start.2 = (bf16[128,1025]{0,1:T(8,128)(2,1)S(1)}, bf16[128,1025]{0,1:T(8,128)(2,1)}, u32[]{:S(2)}) copy-start(bf16[128,1025]{0,1:T(8,128)(2,1)} %param.19) | copy-start | bytes 787204
  252.1 67.1 %all-to-all-start = ((bf16[128,8,1,16,128]{4,3,1,2,0:T(8,128)(2,1)}), bf16[128,8,1,16,128]{4,3,1,2,0:T(8,128)(2,1)}, u32[]{:S(2)}, u32[]{:S(2)}) async-start(bf16[128,8,1,16,128]{4,3,1,2,0:T(8,128)(2,1)} %constant_dynamic-update-slice_fusion.2), calls=%async_computation | async-start | bytes 8388608 | tf_op jit(solution)/shard_map/all_to_all | solution.py:53
  325.5 6.4 %copy-start.4 = (s32[1024]{0:T(1024)S(1)}, s32[1024]{0:T(1024)}, u32[]{:S(2)}) copy-start(s32[1024]{0:T(1024)} %param.16) | copy-start | bytes 12292
